TPU v7x, 32 devices: a whole 2x2x4 slice. The times are simulated.
32 devices in a mesh: dp: 16 (over z, x, core), tensor: 2 (over y).
Axes of the slice: x: 2, y: 2, z: 4, core: 2. Of those that a mesh axis runs over, the one named last changes fastest.
Arguments:
- inputs: bfloat16 [16384, 768], P(('dp', 'tensor')), may hold values from -6 to 6
- lengths: int32 [16], P('dp'), may hold values from 512 to 1024, as said below
- query_weight: bfloat16 [768, 768], P(None, 'tensor'), may hold values from -0.21875 to 0.21875
- query_bias: float32 [768], P('tensor'), may hold values from -3 to 3
- key_weight: bfloat16 [768, 768], P(None, 'tensor'), may hold values from -0.21875 to 0.21875
- value_weight: bfloat16 [768, 768], P(None, 'tensor'), may hold values from -0.21875 to 0.21875
- value_bias: float32 [768], P('tensor'), may hold values from -3 to 3
- proj_weight: bfloat16 [768, 768], P('tensor'), may hold values from -4 to 4
- proj_bias: float32 [768], replicated, may hold values from -3 to 3
- attn_gain: float32 [768], replicated, may hold values from 0.1 to 1.9
- attn_shift: float32 [768], replicated, may hold values from -2 to 2
- up_weight: bfloat16 [768, 3072], P(None, 'tensor'), may hold values from -0.21875 to 0.21875
- up_bias: float32 [3072], P('tensor'), may hold values from -3 to 3
- down_weight: bfloat16 [3072, 768], P('tensor'), may hold values from -0.109375 to 0.109375
- down_bias: float32 [768], replicated, may hold values from -3 to 3
- ffn_gain: float32 [768], replicated, may hold values from 0.1 to 1.9
- ffn_shift: float32 [768], replicated, may hold values from -2 to 2
- filter_couple_scores: float32 [12, 512, 512], P('tensor', 'dp'), may hold values from -5 to 5
- filter_smoothing_jitter: float32 [12, 512, 512], P('tensor', 'dp'), may hold values from -5 to 5
- cotangent: bfloat16 [16384, 768], P(('dp', 'tensor')), may hold values from -6 to 6
Outputs:
- layer_output: bfloat16 [16384, 768], P(('dp', 'tensor'))
- input_grads: bfloat16 [16384, 768], P(('dp', 'tensor'))
- query_grads: float32 [768, 768], P(None, 'tensor')
- key_grads: float32 [768, 768], P(None, 'tensor')
- value_grads: float32 [768, 768], P(None, 'tensor')
- proj_grads: float32 [768, 768], P('tensor')
- up_grads: float32 [768, 3072], P(None, 'tensor')
- down_grads: float32 [3072, 768], P('tensor')
- query_bias_grads: float32 [768], P('tensor')
- value_bias_grads: float32 [768], P('tensor')
- up_bias_grads: float32 [3072], P('tensor')
- proj_bias_grads: float32 [768], replicated
- down_bias_grads: float32 [768], replicated
- attn_gain_grads: float32 [768], replicated
- attn_shift_grads: float32 [768], replicated
- ffn_gain_grads: float32 [768], replicated
- ffn_shift_grads: float32 [768], replicated
- mask_logit_gradients: float32 [12, 512, 512], P('tensor', 'dp')
Inputs may be any that keep to these rules, and one draw needn't show every extreme that they name: Each sequence's live slots are its first lengths[b]; at least one sequence fills all 1024 slots.
All inputs are finite; a program needn't handle non-finite values.
Results may differ from a plain program's by a relative error of at most 0.015.
Values may be sent and summed in bfloat16 or wider, within the bound.
A program may use at most 192 MiB of HBM per device.

v0:
```python
import math
import jax
import jax.numpy as jnp
from jax import lax
from jax.sharding import PartitionSpec as P

HEAD_DIM = 64
softening_heat = 0.5
epsilon = 1e-05


def layer_norm(values, gain, shift):
    centre = values - jnp.mean(values, axis=-1, keepdims=True)
    spread = jnp.mean(centre * centre, axis=-1, keepdims=True)
    inverse = lax.rsqrt(spread + epsilon)
    normal = centre * inverse
    return (normal * gain + shift, normal, inverse)


def norm_back(upstream, normal, inverse, gain):
    scaled = upstream * gain
    first_mean = jnp.mean(scaled, axis=-1, keepdims=True)
    second_mean = jnp.mean(scaled * normal, axis=-1, keepdims=True)
    grad_in = inverse * (scaled - first_mean - normal * second_mean)
    return (grad_in, jnp.sum(upstream * normal, axis=0), jnp.sum(upstream, axis=0))


def on_device(
    inputs,
    lengths,
    query_weight,
    query_bias,
    key_weight,
    value_weight,
    value_bias,
    proj_weight,
    proj_bias,
    attn_gain,
    attn_shift,
    up_weight,
    up_bias,
    down_weight,
    down_bias,
    ffn_gain,
    ffn_shift,
    filter_couple_scores,
    filter_smoothing_jitter,
    cotangent,
):
    rows_half = inputs.shape[0]
    seq_len = rows_half * lax.axis_size("tensor")
    local_width = query_weight.shape[1]
    local_heads = local_width // HEAD_DIM
    window = filter_couple_scores.shape[2]
    blocks = seq_len // window
    score_scale = 1.0 / math.sqrt(HEAD_DIM)
    slot_ids = jnp.arange(seq_len, dtype=jnp.int32)
    live_slots = slot_ids < lengths[0]
    own_live = lax.dynamic_slice_in_dim(live_slots, lax.axis_index("tensor") * rows_half, rows_half)
    softened_filter = jax.nn.sigmoid(
        (filter_couple_scores + filter_smoothing_jitter) / softening_heat
    )
    trainable_focus_filter = lax.all_gather(
        softened_filter.astype(jnp.bfloat16), "dp", axis=1, tiled=True
    )
    full_rows = lax.all_gather(inputs, "tensor", axis=0, tiled=True)
    joint_weight = jnp.concatenate([query_weight, key_weight, value_weight], axis=1)
    joint = jnp.dot(full_rows, joint_weight, preferred_element_type=jnp.float32)
    queries = (joint[:, :local_width] + query_bias).astype(jnp.bfloat16)
    queries = queries.reshape(seq_len, local_heads, HEAD_DIM)
    key_rows = joint[:, local_width : 2 * local_width].astype(jnp.bfloat16)
    key_rows = key_rows.reshape(seq_len, local_heads, HEAD_DIM)
    value_rows = (joint[:, 2 * local_width :] + value_bias).astype(jnp.bfloat16)
    value_rows = value_rows.reshape(seq_len, local_heads, HEAD_DIM)

    def scores_for(query_block):
        scores = (
            jnp.einsum("qhd,khd->hqk", query_block, key_rows, preferred_element_type=jnp.float32)
            * score_scale
        )
        return jnp.where(live_slots[None, None, :], scores, -1e30)

    def apply_mask(softmax_out):
        tiles = (
            softmax_out.reshape(local_heads, window, blocks, window)
            * trainable_focus_filter[:, :, None, :]
        )
        return tiles.reshape(local_heads, window, seq_len)

    def attend(query_block):
        scores = scores_for(query_block)
        row_max = jnp.max(scores, axis=-1)
        exponent = jnp.exp(scores - row_max[..., None])
        row_total = jnp.sum(exponent, axis=-1)
        weighted = apply_mask(exponent / row_total[..., None]).astype(jnp.bfloat16)
        context = jnp.einsum(
            "hqk,khd->qhd", weighted, value_rows, preferred_element_type=jnp.float32
        )
        return (context.astype(jnp.bfloat16), row_max + jnp.log(row_total))

    query_blocks = queries.reshape(blocks, window, local_heads, HEAD_DIM)
    contexts, log_totals = lax.map(attend, query_blocks)
    heads_out = contexts.reshape(seq_len, local_width)
    piece = heads_out
    attn_half = lax.psum_scatter(
        jnp.dot(piece, proj_weight, preferred_element_type=jnp.float32),
        "tensor",
        scatter_dimension=0,
        tiled=True,
    )
    normed, normal_attn, inverse_attn = layer_norm(
        inputs.astype(jnp.float32) + attn_half + proj_bias, attn_gain, attn_shift
    )
    hidden_rows = lax.all_gather(normed.astype(jnp.bfloat16), "tensor", axis=0, tiled=True)
    upper = jnp.dot(hidden_rows, up_weight, preferred_element_type=jnp.float32) + up_bias
    gelu_out, gelu_pull = jax.vjp(lambda given: jax.nn.gelu(given, approximate=False), upper)
    active = gelu_out.astype(jnp.bfloat16)
    piece = active
    ffn_half = lax.psum_scatter(
        jnp.dot(piece, down_weight, preferred_element_type=jnp.float32),
        "tensor",
        scatter_dimension=0,
        tiled=True,
    )
    result, normal_ffn, inverse_ffn = layer_norm(normed + ffn_half + down_bias, ffn_gain, ffn_shift)
    layer_output = result.astype(jnp.bfloat16)
    grad_out = cotangent.astype(jnp.float32) * own_live[:, None].astype(jnp.float32)
    grad_ffn, ffn_gain_grad, ffn_shift_grad = norm_back(grad_out, normal_ffn, inverse_ffn, ffn_gain)
    down_bias_grad = jnp.sum(grad_ffn, axis=0)
    grad_ffn_rows = lax.all_gather(grad_ffn.astype(jnp.bfloat16), "tensor", axis=0, tiled=True)
    down_weight_grad = jnp.einsum(
        "sf,sd->fd", active, grad_ffn_rows, preferred_element_type=jnp.float32
    )
    grad_active = jnp.einsum(
        "sd,fd->sf", grad_ffn_rows, down_weight, preferred_element_type=jnp.float32
    )
    grad_upper = gelu_pull(grad_active)[0].astype(jnp.bfloat16)
    up_bias_grad = jnp.sum(grad_upper, axis=0, dtype=jnp.float32)
    up_weight_grad = jnp.einsum(
        "sd,sf->df", hidden_rows, grad_upper, preferred_element_type=jnp.float32
    )
    piece = grad_upper
    grad_hidden = lax.psum_scatter(
        jnp.einsum("sf,df->sd", piece, up_weight, preferred_element_type=jnp.float32),
        "tensor",
        scatter_dimension=0,
        tiled=True,
    )
    grad_attn, attn_gain_grad, attn_shift_grad = norm_back(
        grad_ffn + grad_hidden, normal_attn, inverse_attn, attn_gain
    )
    proj_bias_grad = jnp.sum(grad_attn, axis=0)
    grad_attn_rows = lax.all_gather(grad_attn.astype(jnp.bfloat16), "tensor", axis=0, tiled=True)
    proj_weight_grad = jnp.einsum(
        "sk,sd->kd", heads_out, grad_attn_rows, preferred_element_type=jnp.float32
    )
    grad_context = jnp.einsum(
        "sd,kd->sk", grad_attn_rows, proj_weight, preferred_element_type=jnp.float32
    ).astype(jnp.bfloat16)

    def attend_back(carry, pieces):
        key_total, value_total, mask_total = carry
        query_block, grad_block, log_block = pieces
        softmax_out = jnp.exp(scores_for(query_block) - log_block[..., None])
        weighted = apply_mask(softmax_out)
        grad_weighted = jnp.einsum(
            "qhd,khd->hqk", grad_block, value_rows, preferred_element_type=jnp.float32
        )
        value_total = value_total + jnp.einsum(
            "hqk,qhd->khd",
            weighted.astype(jnp.bfloat16),
            grad_block,
            preferred_element_type=jnp.float32,
        )
        grad_tiles = grad_weighted.reshape(local_heads, window, blocks, window)
        mask_total = mask_total + jnp.sum(
            grad_tiles * softmax_out.reshape(local_heads, window, blocks, window), axis=2
        )
        grad_softmax = (grad_tiles * trainable_focus_filter[:, :, None, :]).reshape(
            local_heads, window, seq_len
        )
        inner = jnp.sum(grad_weighted * weighted, axis=-1, keepdims=True)
        grad_scores = (softmax_out * (grad_softmax - inner) * score_scale).astype(jnp.bfloat16)
        query_grad = jnp.einsum(
            "hqk,khd->qhd", grad_scores, key_rows, preferred_element_type=jnp.float32
        )
        key_total = key_total + jnp.einsum(
            "hqk,qhd->khd", grad_scores, query_block, preferred_element_type=jnp.float32
        )
        return ((key_total, value_total, mask_total), query_grad.astype(jnp.bfloat16))

    zero_rows = jnp.zeros((seq_len, local_heads, HEAD_DIM), jnp.float32)
    zero_mask = jnp.zeros((local_heads, window, window), jnp.float32)
    (key_total, value_total, mask_total), query_grads = lax.scan(
        attend_back,
        (zero_rows, zero_rows, zero_mask),
        (query_blocks, grad_context.reshape(blocks, window, local_heads, HEAD_DIM), log_totals),
    )
    joint_grad = jnp.concatenate(
        [
            query_grads.reshape(seq_len, local_width),
            key_total.astype(jnp.bfloat16).reshape(seq_len, local_width),
            value_total.astype(jnp.bfloat16).reshape(seq_len, local_width),
        ],
        axis=1,
    )
    joint_weight_grad = jnp.einsum(
        "sd,sk->dk", full_rows, joint_grad, preferred_element_type=jnp.float32
    )
    query_weight_grad = joint_weight_grad[:, :local_width]
    key_weight_grad = joint_weight_grad[:, local_width : 2 * local_width]
    value_weight_grad = joint_weight_grad[:, 2 * local_width :]
    query_bias_grad = jnp.sum(joint_grad[:, :local_width], axis=0, dtype=jnp.float32)
    value_bias_grad = jnp.sum(joint_grad[:, 2 * local_width :], axis=0, dtype=jnp.float32)
    piece = joint_grad
    grad_inputs = lax.psum_scatter(
        jnp.einsum("sk,dk->sd", piece, joint_weight, preferred_element_type=jnp.float32).astype(
            jnp.bfloat16
        ),
        "tensor",
        scatter_dimension=0,
        tiled=True,
    ).astype(jnp.float32)
    input_grads = (grad_attn + grad_inputs).astype(jnp.bfloat16)
    filter_slope_lines = lax.psum_scatter(mask_total, "dp", scatter_dimension=1, tiled=True)
    mask_logit_gradients = (
        filter_slope_lines * softened_filter * (1.0 - softened_filter) / softening_heat
    )
    (
        query_weight_grad,
        key_weight_grad,
        value_weight_grad,
        proj_weight_grad,
        query_bias_grad,
        value_bias_grad,
        up_weight_grad,
        down_weight_grad,
        up_bias_grad,
    ) = lax.psum(
        (
            query_weight_grad,
            key_weight_grad,
            value_weight_grad,
            proj_weight_grad,
            query_bias_grad,
            value_bias_grad,
            up_weight_grad,
            down_weight_grad,
            up_bias_grad,
        ),
        "dp",
    )
    (
        proj_bias_grad,
        down_bias_grad,
        attn_gain_grad,
        attn_shift_grad,
        ffn_gain_grad,
        ffn_shift_grad,
    ) = lax.psum(
        (
            proj_bias_grad,
            down_bias_grad,
            attn_gain_grad,
            attn_shift_grad,
            ffn_gain_grad,
            ffn_shift_grad,
        ),
        ("dp", "tensor"),
    )
    return (
        layer_output,
        input_grads,
        query_weight_grad,
        key_weight_grad,
        value_weight_grad,
        proj_weight_grad,
        up_weight_grad,
        down_weight_grad,
        query_bias_grad,
        value_bias_grad,
        up_bias_grad,
        proj_bias_grad,
        down_bias_grad,
        attn_gain_grad,
        attn_shift_grad,
        ffn_gain_grad,
        ffn_shift_grad,
        mask_logit_gradients,
    )


def solution(mesh):
    in_specs = (
        P(("dp", "tensor"), None),
        P("dp"),
        P(None, "tensor"),
        P("tensor"),
        P(None, "tensor"),
        P(None, "tensor"),
        P("tensor"),
        P("tensor", None),
        P(),
        P(),
        P(),
        P(None, "tensor"),
        P("tensor"),
        P("tensor", None),
        P(),
        P(),
        P(),
        P("tensor", "dp", None),
        P("tensor", "dp", None),
        P(("dp", "tensor"), None),
    )
    out_specs = (
        P(("dp", "tensor"), None),
        P(("dp", "tensor"), None),
        P(None, "tensor"),
        P(None, "tensor"),
        P(None, "tensor"),
        P("tensor", None),
        P(None, "tensor"),
        P("tensor", None),
        P("tensor"),
        P("tensor"),
        P("tensor"),
        P(),
        P(),
        P(),
        P(),
        P(),
        P(),
        P("tensor", "dp", None),
    )
    return jax.shard_map(
        on_device, mesh=mesh, in_specs=in_specs, out_specs=out_specs, check_vma=False
    )
```

profile of v0, /device:TPU:0, one launch (start us, length us, event | category | flops | bytes accessed | tf_op | source)
XLA Modules:
  0.0 1162.9 jit_solution(14874265997577795067)
XLA Ops:
  14.8 24.7 %all-gather.6.cloned.1.call-done = bf16[1024,768]{1,0:T(8,128)(2,1)} async-done(((bf16[512,768]{1,0:T(8,128)(2,1)}), bf16[1024,768]{1,0:T(8,128)(2,1)}) %all-gather.6.cloned.1.call-update) | async-done | bytes 1572880 | tf_op jit(solution)/shard_map/all_gather | solution.py:66
  50.6 37.2 %all-gather.8.cloned.1.call-done = bf16[6,512,512]{2,1,0:T(8,128)(2,1)} async-done(((bf16[6,32,512]{2,1,0:T(8,128)(2,1)}), bf16[6,512,512]{2,1,0:T(8,128)(2,1)}) %all-gather.8.cloned.1.call-update) | async-done | bytes 3145744 | tf_op jit(solution)/shard_map/all_gather | solution.py:63
  88.8 84.2 %while.30 = (s32[]{:T(128)}, bf16[2,512,6,64]{1,3,2,0:T(8,128)(2,1)}, f32[2,6,512]{2,1,0:T(8,128)S(1)}, bf16[2,512,6,64]{1,3,2,0:T(8,128)(2,1)}, bf16[1024,6,64]...) while((s32[]{:T(128)}, ...), condition=%wide.region_3.4_spmd.clone, body=%wide.region_0.3_spmd.clone.sunk | while | flops 846395392 | bytes 103145664 | solution.py:102
  89.4 10.7 mul.485
  100.1 17.0 %mul.486 = f32[6,512,1024]{2,1,0:T(8,128)} reshape(f32[6,512,2,512]{3,2,1,0:T(2,128)} %mul.485) | data formatting | bytes 25165824 | tf_op jit(solution)/shard_map/while/body/eval_jaxpr/mul | solution.py:85
  123.1 6.8 fusion.165
  131.5 10.7 mul.485
  142.2 17.0 %mul.486 = f32[6,512,1024]{2,1,0:T(8,128)} reshape(f32[6,512,2,512]{3,2,1,0:T(2,128)} %mul.485) | data formatting | bytes 25165824 | tf_op jit(solution)/shard_map/while/body/eval_jaxpr/mul | solution.py:85
  165.2 6.8 fusion.165
  179.8 41.9 %reduce-scatter.6.cloned.1.call-done = f32[512,768]{1,0:T(8,128)} async-done(((f32[1024,768]{1,0:T(8,128)}), f32[512,768]{1,0:T(8,128)}) %reduce-scatter.6.cloned.1.call-update) | async-done | bytes 1572880 | tf_op jit(solution)/shard_map/reduce_scatter | solution.py:105
  225.9 27.3 %all-gather.10.cloned.1.call-done = bf16[1024,768]{1,0:T(8,128)(2,1)} async-done(((bf16[512,768]{1,0:T(8,128)(2,1)}), bf16[1024,768]{1,0:T(8,128)(2,1)}) %all-gather.10.cloned.1.call-update) | async-done | bytes 1572880 | tf_op jit(solution)/shard_map/all_gather | solution.py:114
  253.2 18.8 %multiply_convert_fusion.9 = (bf16[1024,1536]{1,0:T(8,128)(2,1)S(1)}, f32[1024,1536]{1,0:T(8,128)}, f32[1024,1536]{1,0:T(8,128)}) fusion(f32[1536]{0:T(1024)S(1)} %copy-done.49, bf16[1024,768]{1,0:T(8,128)(2,1)} %all-gather.10.cloned.1.call-done, bf16[768,1536]{1,0:T(8,128)(2,1)S(1)} %copy-done), kind=kOutput, calls=%fused_computation.61 | convolution fusion | flops 2519728128 | bytes 19666944 | tf_op jit(solution)/shard_map/dot_general | solution.py:115
  273.6 4.3 fusion.98
  278.7 42.8 %reduce-scatter.8.cloned.1.call-done = f32[512,768]{1,0:T(8,128)} async-done(((f32[1024,768]{1,0:T(8,128)}), f32[512,768]{1,0:T(8,128)}) %reduce-scatter.8.cloned.1.call-update) | async-done | bytes 1572880 | tf_op jit(solution)/shard_map/reduce_scatter | solution.py:119
  330.2 27.3 %all-gather.12.cloned.1.call-done = bf16[1024,768]{1,0:T(8,128)(2,1)} async-done(((bf16[512,768]{1,0:T(8,128)(2,1)}), bf16[1024,768]{1,0:T(8,128)(2,1)}) %all-gather.12.cloned.1.call-update) | async-done | bytes 1572880 | tf_op jit(solution)/shard_map/all_gather | solution.py:130
  357.6 10.8 convert_reduce_fusion
  370.0 4.3 fusion.99
  374.4 43.5 %reduce-scatter.10.cloned.1.call-done = f32[512,768]{1,0:T(8,128)} async-done(((f32[1024,768]{1,0:T(8,128)}), f32[512,768]{1,0:T(8,128)}) %reduce-scatter.10.cloned.1.call-update) | async-done | bytes 1572880 | tf_op jit(solution)/shard_map/reduce_scatter | solution.py:143
  425.0 27.3 %all-gather.14.cloned.1.call-done = bf16[1024,768]{1,0:T(8,128)(2,1)} async-done(((bf16[512,768]{1,0:T(8,128)(2,1)}), bf16[1024,768]{1,0:T(8,128)(2,1)}) %all-gather.14.cloned.1.call-update) | async-done | bytes 1572880 | tf_op jit(solution)/shard_map/all_gather | solution.py:153
  464.3 292.9 %while.31 = (s32[]{:T(128)}, f32[1024,6,64]{0,2,1:T(8,128)}, f32[1024,6,64]{0,2,1:T(8,128)S(1)}, f32[6,512,512]{2,1,0:T(8,128)}, bf16[2,512,6,64]{1,3,2,0:T(8,12...) while((s32[]{:T(128)}, f32[1024,6,64]{0,2,1:T(8,128)}, ...), condition=%wide.region_18.19_spmd.clone, body=%wide.region_15.18_spmd.clone.sunk | while | flops 3740476416 | bytes 352058144 | solution.py:194
  467.0 4.5 copy-done.2
  471.5 6.4 fusion.186
  477.9 16.9 %mul.507 = f32[6,512,2,512]{3,2,1,0:T(2,128)} reshape(f32[6,512,1024]{2,1,0:T(8,128)} %fusion.186) | data formatting | bytes 25165824 | tf_op jit(solution)/shard_map/while/body/eval_jaxpr/mul | solution.py:177
  494.8 22.4 %reduce_sum.228 = f32[6,512,512]{2,1,0:T(8,128)} reduce(f32[6,512,2,512]{3,2,1,0:T(2,128)} %mul.507, f32[]{:T(128)} %constant.61.clone.11..sunk), dimensions={2}, to_apply=%region_17.17 | reduce | flops 1572864 | bytes 18874372 | tf_op jit(solution)/shard_map/while/body/eval_jaxpr/reduce_sum | solution.py:176
  517.2 7.2 select_add_fusion.2
  524.4 8.1 mul.505
  532.5 17.0 %mul.506 = f32[6,512,1024]{2,1,0:T(8,128)} reshape(f32[6,512,2,512]{3,2,1,0:T(2,128)} %mul.505) | data formatting | bytes 25165824 | tf_op jit(solution)/shard_map/while/body/eval_jaxpr/mul | solution.py:179
  549.5 24.8 %fusion.187 = bf16[2,512,6,64]{1,3,2,0:T(8,128)(2,1)} fusion(bf16[2,512,6,64]{1,3,2,0:T(8,128)(2,1)} %get-tuple-element.530, s32[]{:T(128)S(6)} %copy.74, bf16[1024,6,64]{0,2,1:T(8,128)(2,1)S(1)} %get-tuple-element.547, f32[6,512,1024]{2,1,0:T(8,128)} %mul.506, f32[6,512,1024]{2,1,0:T(8,128)} %copy-done.2, ...), kind=kOutput, calls=%fused_computation.34.clone.1 | convolution fusion | flops 1249054720 | bytes 53906944 | tf_op jit(solution)/shard_map/while/body/eval_jaxpr/hqk,khd->qhd/dot_general | solution.py:184
  574.3 10.0 bitcast_add_fusion.5
  584.3 25.5 %bitcast_add_fusion.4 = f32[1024,6,64]{0,2,1:T(8,128)} fusion(f32[1024,6,64]{0,2,1:T(8,128)} %get-tuple-element.527, pred[]{:T(512)S(6)} %compare.3, bf16[2,512,6,64]{1,3,2,0:T(8,128)(2,1)S(1)} %get-tuple-element.546, s32[]{:T(128)S(6)} %copy.74, f32[6,512,1024]{2,1,0:T(8,128)} %mul.506, f32[6,512,1024]{2,1,0:T(8,128)} %copy-done.2, ...), kind=kOutput, calls=%fused_computation.30.clone.1 | convolution fusion | flops 1249644544 | bytes 56266752 | tf_op jit(solution)/shard_map/while/body/eval_jaxpr/hqk,qhd->khd/dot_general | solution.py:187
  612.3 4.5 copy-done.2
  616.8 6.4 fusion.186
  623.2 16.9 %mul.507 = f32[6,512,2,512]{3,2,1,0:T(2,128)} reshape(f32[6,512,1024]{2,1,0:T(8,128)} %fusion.186) | data formatting | bytes 25165824 | tf_op jit(solution)/shard_map/while/body/eval_jaxpr/mul | solution.py:177
  640.1 22.4 %reduce_sum.228 = f32[6,512,512]{2,1,0:T(8,128)} reduce(f32[6,512,2,512]{3,2,1,0:T(2,128)} %mul.507, f32[]{:T(128)} %constant.61.clone.11..sunk), dimensions={2}, to_apply=%region_17.17 | reduce | flops 1572864 | bytes 18874372 | tf_op jit(solution)/shard_map/while/body/eval_jaxpr/reduce_sum | solution.py:176
  662.5 9.0 select_add_fusion.2
  671.5 8.1 mul.505
  679.6 17.0 %mul.506 = f32[6,512,1024]{2,1,0:T(8,128)} reshape(f32[6,512,2,512]{3,2,1,0:T(2,128)} %mul.505) | data formatting | bytes 25165824 | tf_op jit(solution)/shard_map/while/body/eval_jaxpr/mul | solution.py:179
  696.6 24.7 %fusion.187 = bf16[2,512,6,64]{1,3,2,0:T(8,128)(2,1)} fusion(bf16[2,512,6,64]{1,3,2,0:T(8,128)(2,1)} %get-tuple-element.530, s32[]{:T(128)S(6)} %copy.74, bf16[1024,6,64]{0,2,1:T(8,128)(2,1)S(1)} %get-tuple-element.547, f32[6,512,1024]{2,1,0:T(8,128)} %mul.506, f32[6,512,1024]{2,1,0:T(8,128)} %copy-done.2, ...), kind=kOutput, calls=%fused_computation.34.clone.1 | convolution fusion | flops 1249054720 | bytes 53906944 | tf_op jit(solution)/shard_map/while/body/eval_jaxpr/hqk,khd->qhd/dot_general | solution.py:184
  721.2 10.0 bitcast_add_fusion.5
  731.3 25.7 %bitcast_add_fusion.4 = f32[1024,6,64]{0,2,1:T(8,128)} fusion(f32[1024,6,64]{0,2,1:T(8,128)} %get-tuple-element.527, pred[]{:T(512)S(6)} %compare.3, bf16[2,512,6,64]{1,3,2,0:T(8,128)(2,1)S(1)} %get-tuple-element.546, s32[]{:T(128)S(6)} %copy.74, f32[6,512,1024]{2,1,0:T(8,128)} %mul.506, f32[6,512,1024]{2,1,0:T(8,128)} %copy-done.2, ...), kind=kOutput, calls=%fused_computation.30.clone.1 | convolution fusion | flops 1249644544 | bytes 56266752 | tf_op jit(solution)/shard_map/while/body/eval_jaxpr/hqk,qhd->khd/dot_general | solution.py:187
  761.2 5.2 convolution_convert_fusion.1
  766.5 7.4 fusion.102
  773.9 4.3 fusion.101
  785.2 40.9 %all-reduce = (f32[768]{0:T(1024)}, f32[768]{0:T(1024)}, f32[768]{0:T(1024)}, f32[768]{0:T(1024)}, f32[768]{0:T(1024)}, /*index=5*/f32[768]{0:T(1024)}) all-reduce(f32[768]{0:T(1024)S(1)} %copy-done.36, f32[768]{0:T(1024)S(1)} %copy-done.35, f32[768]{0:T(1024)S(1)} %copy-done.38, ...), channel_id=1, replica_groups=mesh['dp'=16,'tensor'=2] {'dp','tensor'}, use_global_device_ids=true, to_apply=%region_33.34 | all-reduce | flops 4608 | bytes 36864 | tf_op jit(solution)/shard_map/psum | solution.py:260
  826.5 63.8 %all-reduce.1 = (f32[384]{0:T(512)}, f32[384]{0:T(512)}, f32[1536]{0:T(1024)}) all-reduce(f32[384]{0:T(512)S(1)} %reduce_sum.193, f32[384]{0:T(512)S(1)} %reduce_sum.195, f32[1536]{0:T(1024)S(1)} %copy-done.40), channel_id=1, replica_groups=mesh['dp'=16,'tensor'=2] {'dp'}, use_global_device_ids=true, to_apply=%region_27.28 | all-reduce | flops 2304 | bytes 18432 | tf_op jit(solution)/shard_map/psum | solution.py:239
  892.6 163.7 %all-reduce.5.cloned.1.call-done = (f32[768,384]{0,1:T(8,128)}, f32[768,384]{0,1:T(8,128)}, f32[768,384]{0,1:T(8,128)}, f32[384,768]{1,0:T(8,128)}, f32[768,1536]{1,0:T(8,128)}, /*index=5*/f32[1536,768]{1,0:T(8,128)}) async-done(((f32[768,384]{0,1:T(8,128)}, f32[768,384]{0,1:T(8,128)}, f32[768,384]{0,1:T(8,128)}, f32[384,768]{1,0:T(8,128)}, f32[768,1536]{1,0:T(8,128)}, /*index=5*/f32[1536,768]{1,0:T(8,128)}), ...) | async-done | bytes 14155792 | tf_op jit(solution)/shard_map/psum | solution.py:239
  1063.2 82.3 %reduce-scatter.14.cloned.1.call-done = f32[6,32,512]{2,1,0:T(8,128)} async-done(((f32[6,512,512]{2,1,0:T(8,128)}), f32[6,32,512]{2,1,0:T(8,128)}) %reduce-scatter.14.cloned.1.call-update) | async-done | bytes 393232 | tf_op jit(solution)/shard_map/reduce_scatter | solution.py:225
  1148.4 5.5 copy.92
  (215 shorter events, 107.4 us)
Async XLA Ops:
  7.2 246.0 %copy-start = (bf16[768,1536]{1,0:T(8,128)(2,1)S(1)}, bf16[768,1536]{1,0:T(8,128)(2,1)}, u32[]{:S(2)}) copy-start(bf16[768,1536]{1,0:T(8,128)(2,1)} %param.35) | copy-start | bytes 7077892
  7.2 6.8 copy-start.30
  7.2 32.3 %all-gather.6.cloned.1.call-start = ((), (), s32[]{:S(2)}) async-start(), calls=%async_computation.5 | async-start | bytes 2359296 | tf_op jit(solution)/shard_map/all_gather | solution.py:66
  8.0 79.9 %all-gather.8.cloned.1.call-start = ((), (), s32[]{:S(2)}) async-start(), calls=%async_computation.6 | async-start | bytes 3342336 | tf_op jit(solution)/shard_map/all_gather | solution.py:63
  10.0 211.6 %reduce-scatter.6.cloned.1.call-start = ((), (), s32[]{:S(2)}) async-start(), calls=%async_computation.7 | async-start | bytes 4718592 | tf_op jit(solution)/shard_map/reduce_scatter | solution.py:105
  14.8 28.8 %copy-start.44 = (f32[384]{0:T(512)S(1)}, f32[384]{0:T(512)}, u32[]{:S(2)}) copy-start(f32[384]{0:T(512)} %param.30) | copy-start | bytes 4612
  14.8 28.8 %copy-start.45 = (f32[384]{0:T(512)S(1)}, f32[384]{0:T(512)}, u32[]{:S(2)}) copy-start(f32[384]{0:T(512)} %param.27) | copy-start | bytes 4612
  174.9 46.7 %copy-start.42 = (f32[768]{0:T(1024)S(1)}, f32[768]{0:T(1024)}, u32[]{:S(2)}) copy-start(f32[768]{0:T(1024)} %param.32) | copy-start | bytes 9220
  179.7 45.0 %copy-start.31 = (f32[768]{0:T(1024)S(1)}, f32[768]{0:T(1024)}, u32[]{:S(2)}) copy-start(f32[768]{0:T(1024)} %param.33) | copy-start | bytes 9220
  179.7 45.0 %copy-start.37 = (f32[768]{0:T(1024)S(1)}, f32[768]{0:T(1024)}, u32[]{:S(2)}) copy-start(f32[768]{0:T(1024)} %param.34) | copy-start | bytes 9220
  179.7 73.5 %copy-start.49 = (f32[1536]{0:T(1024)S(1)}, f32[1536]{0:T(1024)}, u32[]{:S(2)}) copy-start(f32[1536]{0:T(1024)} %param.36) | copy-start | bytes 18436
  179.7 73.5 %all-gather.10.cloned.1.call-start = ((), (), s32[]{:S(2)}) async-start(), calls=%async_computation.8 | async-start | bytes 2359296 | tf_op jit(solution)/shard_map/all_gather | solution.py:114
  225.9 95.6 %reduce-scatter.8.cloned.1.call-start = ((), (), s32[]{:S(2)}) async-start(), calls=%async_computation.9 | async-start | bytes 4718592 | tf_op jit(solution)/shard_map/reduce_scatter | solution.py:119
  253.2 20.4 %copy-start.46 = (bf16[1536,768]{1,0:T(8,128)(2,1)S(1)}, bf16[1536,768]{1,0:T(8,128)(2,1)}, u32[]{:S(2)}) copy-start(bf16[1536,768]{1,0:T(8,128)(2,1)} %param.37) | copy-start | bytes 7077892
  273.6 47.9 %copy-start.43 = (f32[768]{0:T(1024)S(1)}, f32[768]{0:T(1024)}, u32[]{:S(2)}) copy-start(f32[768]{0:T(1024)} %param.38) | copy-start | bytes 9220
  277.9 46.5 %copy-start.32 = (f32[768]{0:T(1024)S(1)}, f32[768]{0:T(1024)}, u32[]{:S(2)}) copy-start(f32[768]{0:T(1024)} %param.39) | copy-start | bytes 9220
  277.9 47.9 %copy-start.41 = (f32[768]{0:T(1024)S(1)}, f32[768]{0:T(1024)}, u32[]{:S(2)}) copy-start(f32[768]{0:T(1024)} %param.40) | copy-start | bytes 9220
  277.9 79.6 %all-gather.12.cloned.1.call-start = ((), (), s32[]{:S(2)}) async-start(), calls=%async_computation.10 | async-start | bytes 2359296 | tf_op jit(solution)/shard_map/all_gather | solution.py:130
  330.2 87.7 %reduce-scatter.10.cloned.1.call-start = ((), (), s32[]{:S(2)}) async-start(), calls=%async_computation.11 | async-start | bytes 4718592 | tf_op jit(solution)/shard_map/reduce_scatter | solution.py:143
  374.3 47.4 %copy-start.5 = (f32[512,768]{1,0:T(8,128)S(1)}, f32[512,768]{1,0:T(8,128)}, u32[]{:S(2)}) copy-start(f32[512,768]{1,0:T(8,128)} %copy-done.4) | copy-start | bytes 4718596
  374.3 78.0 %all-gather.14.cloned.1.call-start = ((), (), s32[]{:S(2)}) async-start(), calls=%async_computation.12 | async-start | bytes 2359296 | tf_op jit(solution)/shard_map/all_gather | solution.py:153
  424.9 39.4 %copy-start.6 = (bf16[2,512,6,64]{1,3,2,0:T(8,128)(2,1)S(1)}, bf16[2,512,6,64]{1,3,2,0:T(8,128)(2,1)}, u32[]{:S(2)}) copy-start(bf16[2,512,6,64]{1,3,2,0:T(8,128)(2,1)} %get-tuple-element.601) | copy-start | bytes 2359300
  424.9 465.4 %reduce-scatter.12.cloned.1.call-start = ((), (), s32[]{:S(2)}) async-start(), calls=%async_computation.13 | async-start | bytes 2359296 | tf_op jit(solution)/shard_map/reduce_scatter | solution.py:216
  465.1 6.4 copy-start.7
  465.1 6.4 copy-start.9
  467.0 4.5 copy-start.2
  517.2 7.2 copy-start.3
  610.4 6.4 copy-start.7
  610.4 6.4 copy-start.9
  612.3 4.5 copy-start.2
  662.5 9.0 copy-start.3
  761.2 5.2 copy-start.28
  766.4 7.4 copy-start.21
  766.4 289.9 %all-reduce.5.cloned.1.call-start = ((), (), s32[]{:S(2)}) async-start(), calls=%async_computation.15 | async-start | bytes 28311552 | tf_op jit(solution)/shard_map/psum | solution.py:239
  766.5 7.4 copy-start.18
  773.9 4.3 copy-start.20
  773.9 4.3 copy-start.48
  784.4 41.8 %copy-start.13 = (bf16[2,512,6,64]{1,3,2,0:T(8,128)(2,1)S(1)}, bf16[2,512,6,64]{1,3,2,0:T(8,128)(2,1)}, u32[]{:S(2)}) copy-start(bf16[2,512,6,64]{1,3,2,0:T(8,128)(2,1)} %get-tuple-element.128) | copy-start | bytes 2359300
  784.4 42.1 %copy-start.40 = (f32[1536]{0:T(1024)S(1)}, f32[1536]{0:T(1024)}, u32[]{:S(2)}) copy-start(f32[1536]{0:T(1024)} %get-tuple-element.336) | copy-start | bytes 18436
  784.4 105.9 %copy-start.11 = (f32[512,768]{1,0:T(8,128)S(1)}, f32[512,768]{1,0:T(8,128)}, u32[]{:S(2)}) copy-start(f32[512,768]{1,0:T(8,128)} %copy-done.10) | copy-start | bytes 4718596
  784.4 361.1 %reduce-scatter.14.cloned.1.call-start = ((), (), s32[]{:S(2)}) async-start(), calls=%async_computation.14 | async-start | bytes 6684672 | tf_op jit(solution)/shard_map/reduce_scatter | solution.py:225
  890.4 255.2 %copy-start.22 = (f32[6,32,512]{2,1,0:T(8,128)S(1)}, f32[6,32,512]{2,1,0:T(8,128)}, u32[]{:S(2)}) copy-start(f32[6,32,512]{2,1,0:T(8,128)} %param.41) | copy-start | bytes 1179652
  890.4 255.2 %copy-start.23 = (f32[6,32,512]{2,1,0:T(8,128)S(1)}, f32[6,32,512]{2,1,0:T(8,128)}, u32[]{:S(2)}) copy-start(f32[6,32,512]{2,1,0:T(8,128)} %param.42) | copy-start | bytes 1179652
  1056.3 5.5 copy-start.25
  1056.3 91.1 %copy-start.24 = (f32[384,768]{1,0:T(8,128)S(1)}, f32[384,768]{1,0:T(8,128)}, u32[]{:S(2)}) copy-start(f32[384,768]{1,0:T(8,128)} %get-tuple-element.561) | copy-start | bytes 3538948
  1147.4 6.5 slice-start
  1148.4 5.5 slice-start.1
  1148.4 7.7 copy-start.1
  (23 other events, 38.0 us)
Sparse Core Ops, SparseCore 0:
  9.6 29.8 all-gather.5
  42.3 45.4 all-gather.7
  179.8 41.7 reduce-scatter.5
  226.0 27.1 all-gather.9
  278.0 43.3 reduce-scatter.7
  330.3 27.1 all-gather.11
  374.4 43.4 reduce-scatter.9
  425.0 27.1 all-gather.13
  766.5 26.1 reduce-scatter.11
  798.3 258.0 all-reduce.4
  1060.3 85.1 reduce-scatter.13
where the time goes:
time: 1170 us; the launch traced here: 1160 us
  waiting for transfers between devices  519 us (44%)
  matrix products  227 us (19%)
  local copies, waits for them, and re-layouts  200 us (17%)
  blocking collectives  105 us (9%)
  other arithmetic  95.9 us (8%)
  between operations  15.2 us (1%)
    psum x1, waiting for transfers between devices, on_device(): lax.psum((query_weight_grad, key_weight_grad, value_weight_grad, proj_wei...  164 us
    reduce_scatter x1, waiting for transfers between devices, on_device(): lax.psum_scatter(mask_total, 'dp', scatter_dimension=1, tiled=True)  82.3 us
    psum x1, blocking collectives, on_device(): lax.psum((query_weight_grad, key_weight_grad, value_weight_grad, proj_wei...  63.8 us
    mul x4, local copies, waits for them, and re-layouts, apply_mask(): softmax_out.reshape(local_heads, window, blocks, window)  55.4 us
    dot_general x2, matrix products, attend_back(): jnp.einsum('hqk,qhd->khd', grad_scores, query_block, preferred_element_ty...  51.1 us
    mul x4, local copies, waits for them, and re-layouts, attend_back(): grad_tiles * trainable_focus_filter[:, :, None, :]  50.1 us
    dot_general x2, matrix products, attend_back(): jnp.einsum('hqk,khd->qhd', grad_scores, key_rows, preferred_element_type=...  49.5 us
    reduce_sum x2, other arithmetic, attend_back(): jnp.sum(grad_tiles * softmax_out.reshape(local_heads, window, blocks, win...  44.8 us
  transfers between devices with their start and end apart: 11, of which 10 were waited for; matrix products, arithmetic and copies ran while one was open for 4% of the time, Pallas kernels for 0%

commit v1 on v0

--- a/solution.py
+++ b/solution.py
@@ -7,6 +7,31 @@
 HEAD_DIM = 64
 softening_heat = 0.5
 epsilon = 1e-05
+
+
+def choose_tiles(raw, where_dim):
+    raw = jnp.moveaxis(raw, 0, where_dim)
+    field_out = raw.shape
+    all_rows = raw.reshape(
+        *field_out[:where_dim],
+        field_out[where_dim] * field_out[where_dim + 1],
+        *field_out[where_dim + 2 :]
+    )
+    return all_rows
+
+
+def choose_sectors(mine_x, row_axis):
+    wide_n = lax.axis_size(row_axis)
+    finding = mine_x[None]
+    for at in range(wide_n.bit_length() - 1):
+        r_now = 1 << at
+        kept_arr = tuple(((t, t ^ r_now) for t in range(wide_n)))
+        f_now = lax.ppermute(finding, axis_name=row_axis, perm=kept_arr)
+        y_new = jnp.stack([finding, f_now], 0)
+        aux = lax.axis_index(row_axis)
+        item_now = aux >> at & 1
+        finding = jnp.where(item_now == 0, y_new, y_new[::-1]).reshape(-1, *mine_x.shape)
+    return finding
 
 
 def layer_norm(values, gain, shift):
@@ -63,7 +88,8 @@
     trainable_focus_filter = lax.all_gather(
         softened_filter.astype(jnp.bfloat16), "dp", axis=1, tiled=True
     )
-    full_rows = lax.all_gather(inputs, "tensor", axis=0, tiled=True)
+    parts_out = choose_sectors(inputs, "tensor")
+    full_rows = choose_tiles(parts_out, 0)
     joint_weight = jnp.concatenate([query_weight, key_weight, value_weight], axis=1)
     joint = jnp.dot(full_rows, joint_weight, preferred_element_type=jnp.float32)
     queries = (joint[:, :local_width] + query_bias).astype(jnp.bfloat16)

time: 1170 us -> 1140 us (0.974)
  waiting for transfers between devices: 519 us -> 488 us
    psum x1, waiting for transfers between devices: 164 us -> 251 us  [on_device(): lax.psum((query_weight_grad, key_weight_grad, value_weight_grad, proj_wei...]
    reduce_scatter x1, waiting for transfers between devices: 82.3 us -> 0.01 us  [on_device(): lax.psum_scatter(mask_total, 'dp', scatter_dimension=1, tiled=True)]
    all_gather x1, waiting for transfers between devices: 37.2 us -> 12.1 us  [on_device(): lax.all_gather(softened_filter.astype(jnp.bfloat16), 'dp', axis=1, tiled=...]
    all_gather x1 -> x0, waiting for transfers between devices: 24.7 us -> none  [on_device(): full_rows = lax.all_gather(inputs, 'tensor', axis=0, tiled=True)]
    ppermute x0 -> x1, waiting for transfers between devices: none -> 14.4 us  [choose_sectors(): f_now = lax.ppermute(finding, axis_name=row_axis, perm=kept_arr)]
    unnamed x104 -> x112, local copies, waits for them, and re-layouts: 31.7 us -> 28.2 us
  transfers between devices with their start and end apart: 11 -> 11, of which waited for: 10 -> 9; matrix products, arithmetic and copies ran while one was open for 4% -> 4% of each run, Pallas kernels for 0% -> 0%
where the time goes in v1:
time: 1140 us; the launch traced here: 1130 us
  waiting for transfers between devices  488 us (43%)
  matrix products  224 us (20%)
  local copies, waits for them, and re-layouts  202 us (18%)
  blocking collectives  102 us (9%)
  other arithmetic  97.5 us (9%)
  between operations  15.5 us (1%)
    psum x1, waiting for transfers between devices, on_device(): lax.psum((query_weight_grad, key_weight_grad, value_weight_grad, proj_wei...  251 us
    psum x1, blocking collectives, on_device(): lax.psum((query_weight_grad, key_weight_grad, value_weight_grad, proj_wei...  62.5 us
    mul x4, local copies, waits for them, and re-layouts, apply_mask(): softmax_out.reshape(local_heads, window, blocks, window)  55.4 us
    dot_general x2, matrix products, attend_back(): jnp.einsum('hqk,qhd->khd', grad_scores, query_block, preferred_element_ty...  50.6 us
    mul x4, local copies, waits for them, and re-layouts, attend_back(): grad_tiles * trainable_focus_filter[:, :, None, :]  50.1 us
    dot_general x2, matrix products, attend_back(): jnp.einsum('hqk,khd->qhd', grad_scores, key_rows, preferred_element_type=...  48.4 us
    reduce_sum x2, other arithmetic, attend_back(): jnp.sum(grad_tiles * softmax_out.reshape(local_heads, window, blocks, win...  44.8 us
    reduce_scatter x1, waiting for transfers between devices, on_device(): lax.psum_scatter(jnp.einsum('sf,df->sd', piece, up_weight, preferred_elem...  43.5 us
  transfers between devices with their start and end apart: 11, of which 9 were waited for; matrix products, arithmetic and copies ran while one was open for 4% of the time, Pallas kernels for 0%

profile of v1, /device:TPU:0, one launch (start us, length us, event | category | flops | bytes accessed | tf_op | source)
XLA Modules:
  0.0 1133.8 jit_solution(2999398556807573448)
XLA Ops:
  16.0 14.4 %collective-permute-done = bf16[1,512,768]{2,1,0:T(8,128)(2,1)} collective-permute-done((bf16[1,512,768]{2,1,0:T(8,128)(2,1)}, bf16[1,512,768]{2,1,0:T(8,128)(2,1)}, u32[]{:S(2)}, u32[]{:S(2)}) %collective-permute-start) | collective-permute-done | bytes 786464 | tf_op jit(solution)/shard_map/ppermute | solution.py:29
  46.8 12.1 %all-gather.5.cloned.1.call-done = bf16[6,512,512]{2,1,0:T(8,128)(2,1)} async-done(((bf16[6,32,512]{2,1,0:T(8,128)(2,1)}), bf16[6,512,512]{2,1,0:T(8,128)(2,1)}) %all-gather.5.cloned.1.call-update) | async-done | bytes 3145744 | tf_op jit(solution)/shard_map/all_gather | solution.py:88
  59.8 84.2 %while.30 = (s32[]{:T(128)}, bf16[2,512,6,64]{1,3,2,0:T(8,128)(2,1)}, f32[2,6,512]{2,1,0:T(8,128)S(1)}, bf16[2,512,6,64]{1,3,2,0:T(8,128)(2,1)}, bf16[1024,6,64]...) while((s32[]{:T(128)}, ...), condition=%wide.region_3.4_spmd.clone, body=%wide.region_0.3_spmd.clone.sunk | while | flops 846395392 | bytes 103145664 | solution.py:128
  60.5 10.7 mul.485
  71.2 17.0 %mul.486 = f32[6,512,1024]{2,1,0:T(8,128)} reshape(f32[6,512,2,512]{3,2,1,0:T(2,128)} %mul.485) | data formatting | bytes 25165824 | tf_op jit(solution)/shard_map/while/body/eval_jaxpr/mul | solution.py:111
  94.2 6.8 fusion.167
  102.6 10.7 mul.485
  113.3 17.0 %mul.486 = f32[6,512,1024]{2,1,0:T(8,128)} reshape(f32[6,512,2,512]{3,2,1,0:T(2,128)} %mul.485) | data formatting | bytes 25165824 | tf_op jit(solution)/shard_map/while/body/eval_jaxpr/mul | solution.py:111
  136.3 6.8 fusion.167
  147.0 3.7 fusion.99
  150.9 41.9 %reduce-scatter.6.cloned.1.call-done = f32[512,768]{1,0:T(8,128)} async-done(((f32[1024,768]{1,0:T(8,128)}), f32[512,768]{1,0:T(8,128)}) %reduce-scatter.6.cloned.1.call-update) | async-done | bytes 1572880 | tf_op jit(solution)/shard_map/reduce_scatter | solution.py:131
  197.0 27.3 %all-gather.7.cloned.1.call-done = bf16[1024,768]{1,0:T(8,128)(2,1)} async-done(((bf16[512,768]{1,0:T(8,128)(2,1)}), bf16[1024,768]{1,0:T(8,128)(2,1)}) %all-gather.7.cloned.1.call-update) | async-done | bytes 1572880 | tf_op jit(solution)/shard_map/all_gather | solution.py:140
  224.3 18.8 %multiply_convert_fusion.9 = (bf16[1024,1536]{1,0:T(8,128)(2,1)S(1)}, f32[1024,1536]{1,0:T(8,128)}, f32[1024,1536]{1,0:T(8,128)}) fusion(f32[1536]{0:T(1024)S(1)} %copy-done.52, bf16[1024,768]{1,0:T(8,128)(2,1)} %all-gather.7.cloned.1.call-done, bf16[768,1536]{1,0:T(8,128)(2,1)S(1)} %copy-done), kind=kOutput, calls=%fused_computation.61 | convolution fusion | flops 2519728128 | bytes 19666944 | tf_op jit(solution)/shard_map/dot_general | solution.py:141
  244.7 4.3 fusion.100
  249.8 42.8 %reduce-scatter.8.cloned.1.call-done = f32[512,768]{1,0:T(8,128)} async-done(((f32[1024,768]{1,0:T(8,128)}), f32[512,768]{1,0:T(8,128)}) %reduce-scatter.8.cloned.1.call-update) | async-done | bytes 1572880 | tf_op jit(solution)/shard_map/reduce_scatter | solution.py:145
  301.3 27.3 %all-gather.9.cloned.1.call-done = bf16[1024,768]{1,0:T(8,128)(2,1)} async-done(((bf16[512,768]{1,0:T(8,128)(2,1)}), bf16[1024,768]{1,0:T(8,128)(2,1)}) %all-gather.9.cloned.1.call-update) | async-done | bytes 1572880 | tf_op jit(solution)/shard_map/all_gather | solution.py:156
  328.6 10.8 convert_reduce_fusion
  341.1 4.3 fusion.101
  345.5 43.5 %reduce-scatter.10.cloned.1.call-done = f32[512,768]{1,0:T(8,128)} async-done(((f32[1024,768]{1,0:T(8,128)}), f32[512,768]{1,0:T(8,128)}) %reduce-scatter.10.cloned.1.call-update) | async-done | bytes 1572880 | tf_op jit(solution)/shard_map/reduce_scatter | solution.py:169
  389.0 3.8 multiply_reduce_fusion.2
  396.1 27.3 %all-gather.11.cloned.1.call-done = bf16[1024,768]{1,0:T(8,128)(2,1)} async-done(((bf16[512,768]{1,0:T(8,128)(2,1)}), bf16[1024,768]{1,0:T(8,128)(2,1)}) %all-gather.11.cloned.1.call-update) | async-done | bytes 1572880 | tf_op jit(solution)/shard_map/all_gather | solution.py:179
  423.4 3.4 convolution_convert_fusion.2
  435.4 293.5 %while.31 = (s32[]{:T(128)}, f32[1024,6,64]{0,2,1:T(8,128)}, f32[1024,6,64]{0,2,1:T(8,128)S(1)}, f32[6,512,512]{2,1,0:T(8,128)}, bf16[2,512,6,64]{1,3,2,0:T(8,12...) while((s32[]{:T(128)}, f32[1024,6,64]{0,2,1:T(8,128)}, ...), condition=%wide.region_18.19_spmd.clone, body=%wide.region_15.18_spmd.clone.sunk | while | flops 3740476416 | bytes 348912384 | solution.py:220
  439.1 4.5 copy-done.2
  443.7 6.4 fusion.188
  450.1 16.9 %mul.507 = f32[6,512,2,512]{3,2,1,0:T(2,128)} reshape(f32[6,512,1024]{2,1,0:T(8,128)} %fusion.188) | data formatting | bytes 25165824 | tf_op jit(solution)/shard_map/while/body/eval_jaxpr/mul | solution.py:203
  467.0 22.4 %reduce_sum.228 = f32[6,512,512]{2,1,0:T(8,128)} reduce(f32[6,512,2,512]{3,2,1,0:T(2,128)} %mul.507, f32[]{:T(128)} %constant.62.clone.11..sunk), dimensions={2}, to_apply=%region_17.17 | reduce | flops 1572864 | bytes 18874372 | tf_op jit(solution)/shard_map/while/body/eval_jaxpr/reduce_sum | solution.py:202
  489.4 7.2 select_add_fusion.2
  496.6 8.1 mul.505
  504.7 17.0 %mul.506 = f32[6,512,1024]{2,1,0:T(8,128)} reshape(f32[6,512,2,512]{3,2,1,0:T(2,128)} %mul.505) | data formatting | bytes 25165824 | tf_op jit(solution)/shard_map/while/body/eval_jaxpr/mul | solution.py:205
  521.7 24.2 %fusion.189 = bf16[2,512,6,64]{1,3,2,0:T(8,128)(2,1)} fusion(bf16[2,512,6,64]{1,3,2,0:T(8,128)(2,1)} %get-tuple-element.494, s32[]{:T(128)S(6)} %copy.75, bf16[1024,6,64]{0,2,1:T(8,128)(2,1)S(1)} %get-tuple-element.511, f32[6,512,1024]{2,1,0:T(8,128)} %mul.506, f32[6,512,1024]{2,1,0:T(8,128)} %copy-done.2, ...), kind=kOutput, calls=%fused_computation.34.clone.1 | convolution fusion | flops 1249054720 | bytes 53906944 | tf_op jit(solution)/shard_map/while/body/eval_jaxpr/hqk,khd->qhd/dot_general | solution.py:210
  545.9 10.0 bitcast_add_fusion.5
  555.9 25.1 %bitcast_add_fusion.4 = f32[1024,6,64]{0,2,1:T(8,128)} fusion(f32[1024,6,64]{0,2,1:T(8,128)} %get-tuple-element.491, pred[]{:T(512)S(6)} %compare.3, bf16[2,512,6,64]{1,3,2,0:T(8,128)(2,1)} %get-tuple-element.510, s32[]{:T(128)S(6)} %copy.75, f32[6,512,1024]{2,1,0:T(8,128)} %mul.506, f32[6,512,1024]{2,1,0:T(8,128)} %copy-done.2, ...), kind=kOutput, calls=%fused_computation.30.clone.1 | convolution fusion | flops 1249644544 | bytes 56266752 | tf_op jit(solution)/shard_map/while/body/eval_jaxpr/hqk,qhd->khd/dot_general | solution.py:213
  584.7 4.5 copy-done.2
  589.2 6.4 fusion.188
  595.6 16.9 %mul.507 = f32[6,512,2,512]{3,2,1,0:T(2,128)} reshape(f32[6,512,1024]{2,1,0:T(8,128)} %fusion.188) | data formatting | bytes 25165824 | tf_op jit(solution)/shard_map/while/body/eval_jaxpr/mul | solution.py:203
  612.5 22.4 %reduce_sum.228 = f32[6,512,512]{2,1,0:T(8,128)} reduce(f32[6,512,2,512]{3,2,1,0:T(2,128)} %mul.507, f32[]{:T(128)} %constant.62.clone.11..sunk), dimensions={2}, to_apply=%region_17.17 | reduce | flops 1572864 | bytes 18874372 | tf_op jit(solution)/shard_map/while/body/eval_jaxpr/reduce_sum | solution.py:202
  634.9 9.0 select_add_fusion.2
  643.9 8.1 mul.505
  652.0 17.0 %mul.506 = f32[6,512,1024]{2,1,0:T(8,128)} reshape(f32[6,512,2,512]{3,2,1,0:T(2,128)} %mul.505) | data formatting | bytes 25165824 | tf_op jit(solution)/shard_map/while/body/eval_jaxpr/mul | solution.py:205
  669.0 24.2 %fusion.189 = bf16[2,512,6,64]{1,3,2,0:T(8,128)(2,1)} fusion(bf16[2,512,6,64]{1,3,2,0:T(8,128)(2,1)} %get-tuple-element.494, s32[]{:T(128)S(6)} %copy.75, bf16[1024,6,64]{0,2,1:T(8,128)(2,1)S(1)} %get-tuple-element.511, f32[6,512,1024]{2,1,0:T(8,128)} %mul.506, f32[6,512,1024]{2,1,0:T(8,128)} %copy-done.2, ...), kind=kOutput, calls=%fused_computation.34.clone.1 | convolution fusion | flops 1249054720 | bytes 53906944 | tf_op jit(solution)/shard_map/while/body/eval_jaxpr/hqk,khd->qhd/dot_general | solution.py:210
  693.2 10.0 bitcast_add_fusion.5
  703.2 25.5 %bitcast_add_fusion.4 = f32[1024,6,64]{0,2,1:T(8,128)} fusion(f32[1024,6,64]{0,2,1:T(8,128)} %get-tuple-element.491, pred[]{:T(512)S(6)} %compare.3, bf16[2,512,6,64]{1,3,2,0:T(8,128)(2,1)} %get-tuple-element.510, s32[]{:T(128)S(6)} %copy.75, f32[6,512,1024]{2,1,0:T(8,128)} %mul.506, f32[6,512,1024]{2,1,0:T(8,128)} %copy-done.2, ...), kind=kOutput, calls=%fused_computation.30.clone.1 | convolution fusion | flops 1249644544 | bytes 56266752 | tf_op jit(solution)/shard_map/while/body/eval_jaxpr/hqk,qhd->khd/dot_general | solution.py:213
  737.4 7.4 fusion.104
  744.7 4.3 fusion.103
  756.2 39.9 %all-reduce = (f32[768]{0:T(1024)}, f32[768]{0:T(1024)}, f32[768]{0:T(1024)}, f32[768]{0:T(1024)}, f32[768]{0:T(1024)}, /*index=5*/f32[768]{0:T(1024)}) all-reduce(f32[768]{0:T(1024)S(1)} %copy-done.40, f32[768]{0:T(1024)S(1)} %copy-done.39, f32[768]{0:T(1024)S(1)} %copy-done.42, ...), channel_id=1, replica_groups=mesh['dp'=16,'tensor'=2] {'dp','tensor'}, use_global_device_ids=true, to_apply=%region_33.34 | all-reduce | flops 4608 | bytes 36864 | tf_op jit(solution)/shard_map/psum | solution.py:286
  796.5 62.5 %all-reduce.1 = (f32[384]{0:T(512)}, f32[384]{0:T(512)}, f32[1536]{0:T(1024)}) all-reduce(f32[384]{0:T(512)S(1)} %reduce_sum.193, f32[384]{0:T(512)S(1)} %reduce_sum.195, f32[1536]{0:T(1024)S(1)} %copy-done.44), channel_id=1, replica_groups=mesh['dp'=16,'tensor'=2] {'dp'}, use_global_device_ids=true, to_apply=%region_27.28 | all-reduce | flops 2304 | bytes 18432 | tf_op jit(solution)/shard_map/psum | solution.py:265
  863.0 250.7 %all-reduce.5.cloned.1.call-done = (f32[768,384]{1,0:T(8,128)}, f32[768,384]{1,0:T(8,128)}, f32[768,384]{1,0:T(8,128)}, f32[384,768]{1,0:T(8,128)}, f32[768,1536]{1,0:T(8,128)}, /*index=5*/f32[1536,768]{1,0:T(8,128)}) async-done(((f32[768,384]{1,0:T(8,128)}, f32[768,384]{1,0:T(8,128)}, f32[768,384]{1,0:T(8,128)}, f32[384,768]{1,0:T(8,128)}, f32[768,1536]{1,0:T(8,128)}, /*index=5*/f32[1536,768]{1,0:T(8,128)}), ...) | async-done | bytes 14155792 | tf_op jit(solution)/shard_map/psum | solution.py:265
  (223 shorter events, 112.3 us)
Async XLA Ops:
  7.2 217.1 %copy-start = (bf16[768,1536]{1,0:T(8,128)(2,1)S(1)}, bf16[768,1536]{1,0:T(8,128)(2,1)}, u32[]{:S(2)}) copy-start(bf16[768,1536]{1,0:T(8,128)(2,1)} %param.35) | copy-start | bytes 7077892
  7.2 23.2 %copy-start.19 = (bf16[512,768]{1,0:T(8,128)(2,1)S(1)}, bf16[512,768]{1,0:T(8,128)(2,1)}, u32[]{:S(2)}) copy-start(bf16[512,768]{1,0:T(8,128)(2,1)} %param.24) | copy-start | bytes 2359300
  7.2 51.7 %all-gather.5.cloned.1.call-start = ((), (), s32[]{:S(2)}) async-start(), calls=%async_computation.5 | async-start | bytes 3342336 | tf_op jit(solution)/shard_map/all_gather | solution.py:88
  9.4 183.4 %reduce-scatter.6.cloned.1.call-start = ((), (), s32[]{:S(2)}) async-start(), calls=%async_computation.6 | async-start | bytes 4718592 | tf_op jit(solution)/shard_map/reduce_scatter | solution.py:131
  9.4 20.9 %collective-permute-start = (bf16[1,512,768]{2,1,0:T(8,128)(2,1)}, bf16[1,512,768]{2,1,0:T(8,128)(2,1)}, u32[]{:S(2)}, u32[]{:S(2)}) collective-permute-start(bf16[1,512,768]{2,1,0:T(8,128)(2,1)} %bitcast.158), channel_id=1, source_target_pairs={{0,1},{1,0},{2,3},{3,2},{4,5},{5,4},{6,7},{7,6},{8,9},{9,8},{10,11... | collective-permute-start | bytes 2359304 | tf_op jit(solution)/shard_map/ppermute | solution.py:29
  15.9 18.3 %copy-start.33 = (bf16[768,1152]{1,0:T(8,128)(2,1)}, bf16[768,1152]{1,0:T(8,128)(2,1)S(1)}, u32[]{:S(2)}) copy-start(bf16[768,1152]{1,0:T(8,128)(2,1)S(1)} %constant_dynamic-update-slice_fusion) | copy-start | bytes 5308420
  32.0 3.2 copy-start.48
  146.0 46.7 %copy-start.46 = (f32[768]{0:T(1024)S(1)}, f32[768]{0:T(1024)}, u32[]{:S(2)}) copy-start(f32[768]{0:T(1024)} %param.32) | copy-start | bytes 9220
  150.8 45.0 %copy-start.35 = (f32[768]{0:T(1024)S(1)}, f32[768]{0:T(1024)}, u32[]{:S(2)}) copy-start(f32[768]{0:T(1024)} %param.33) | copy-start | bytes 9220
  150.8 45.0 %copy-start.41 = (f32[768]{0:T(1024)S(1)}, f32[768]{0:T(1024)}, u32[]{:S(2)}) copy-start(f32[768]{0:T(1024)} %param.34) | copy-start | bytes 9220
  150.8 73.5 %copy-start.52 = (f32[1536]{0:T(1024)S(1)}, f32[1536]{0:T(1024)}, u32[]{:S(2)}) copy-start(f32[1536]{0:T(1024)} %param.36) | copy-start | bytes 18436
  150.8 73.5 %all-gather.7.cloned.1.call-start = ((), (), s32[]{:S(2)}) async-start(), calls=%async_computation.7 | async-start | bytes 2359296 | tf_op jit(solution)/shard_map/all_gather | solution.py:140
  197.0 95.6 %reduce-scatter.8.cloned.1.call-start = ((), (), s32[]{:S(2)}) async-start(), calls=%async_computation.8 | async-start | bytes 4718592 | tf_op jit(solution)/shard_map/reduce_scatter | solution.py:145
  224.3 20.4 %copy-start.50 = (bf16[1536,768]{1,0:T(8,128)(2,1)S(1)}, bf16[1536,768]{1,0:T(8,128)(2,1)}, u32[]{:S(2)}) copy-start(bf16[1536,768]{1,0:T(8,128)(2,1)} %param.37) | copy-start | bytes 7077892
  244.7 47.9 %copy-start.47 = (f32[768]{0:T(1024)S(1)}, f32[768]{0:T(1024)}, u32[]{:S(2)}) copy-start(f32[768]{0:T(1024)} %param.38) | copy-start | bytes 9220
  249.0 46.5 %copy-start.36 = (f32[768]{0:T(1024)S(1)}, f32[768]{0:T(1024)}, u32[]{:S(2)}) copy-start(f32[768]{0:T(1024)} %param.39) | copy-start | bytes 9220
  249.0 47.9 %copy-start.45 = (f32[768]{0:T(1024)S(1)}, f32[768]{0:T(1024)}, u32[]{:S(2)}) copy-start(f32[768]{0:T(1024)} %param.40) | copy-start | bytes 9220
  249.0 79.6 %all-gather.9.cloned.1.call-start = ((), (), s32[]{:S(2)}) async-start(), calls=%async_computation.9 | async-start | bytes 2359296 | tf_op jit(solution)/shard_map/all_gather | solution.py:156
  301.3 87.7 %reduce-scatter.10.cloned.1.call-start = ((), (), s32[]{:S(2)}) async-start(), calls=%async_computation.10 | async-start | bytes 4718592 | tf_op jit(solution)/shard_map/reduce_scatter | solution.py:169
  345.4 47.4 %copy-start.5 = (f32[512,768]{1,0:T(8,128)S(1)}, f32[512,768]{1,0:T(8,128)}, u32[]{:S(2)}) copy-start(f32[512,768]{1,0:T(8,128)} %copy-done.4) | copy-start | bytes 4718596
  345.4 77.9 %all-gather.11.cloned.1.call-start = ((), (), s32[]{:S(2)}) async-start(), calls=%async_computation.11 | async-start | bytes 2359296 | tf_op jit(solution)/shard_map/all_gather | solution.py:179
  396.0 39.4 %copy-start.7 = (bf16[1024,6,64]{0,2,1:T(8,128)(2,1)S(1)}, bf16[1024,6,64]{0,2,1:T(8,128)(2,1)}, u32[]{:S(2)}) copy-start(bf16[1024,6,64]{0,2,1:T(8,128)(2,1)} %get-tuple-element.564) | copy-start | bytes 2359300
  396.0 463.0 %reduce-scatter.12.cloned.1.call-start = ((), (), s32[]{:S(2)}) async-start(), calls=%async_computation.12 | async-start | bytes 2359296 | tf_op jit(solution)/shard_map/reduce_scatter | solution.py:242
  436.2 7.5 copy-start.8
  439.1 4.5 copy-start.2
  489.4 7.2 copy-start.3
  581.7 7.5 copy-start.8
  584.7 4.5 copy-start.2
  634.9 9.0 copy-start.3
  728.9 4.2 copy-start.34
  733.1 3.4 copy-start.31
  736.6 124.6 %reduce-scatter.14.cloned.1.call-start = ((), (), s32[]{:S(2)}) async-start(), calls=%async_computation.13 | async-start | bytes 6684672 | tf_op jit(solution)/shard_map/reduce_scatter | solution.py:251
  737.3 7.4 copy-start.22
  737.3 376.5 %all-reduce.5.cloned.1.call-start = ((), (), s32[]{:S(2)}) async-start(), calls=%async_computation.14 | async-start | bytes 28311552 | tf_op jit(solution)/shard_map/psum | solution.py:265
  737.3 7.4 copy-start.18
  744.7 4.3 copy-start.21
  744.7 4.3 copy-start.51
  755.5 40.7 %copy-start.12 = (bf16[2,512,6,64]{1,3,2,0:T(8,128)(2,1)S(1)}, bf16[2,512,6,64]{1,3,2,0:T(8,128)(2,1)}, u32[]{:S(2)}) copy-start(bf16[2,512,6,64]{1,3,2,0:T(8,128)(2,1)} %get-tuple-element.128) | copy-start | bytes 2359300
  755.5 41.0 %copy-start.44 = (f32[1536]{0:T(1024)S(1)}, f32[1536]{0:T(1024)}, u32[]{:S(2)}) copy-start(f32[1536]{0:T(1024)} %get-tuple-element.300) | copy-start | bytes 18436
  755.5 103.5 %copy-start.10 = (f32[512,768]{1,0:T(8,128)S(1)}, f32[512,768]{1,0:T(8,128)}, u32[]{:S(2)}) copy-start(f32[512,768]{1,0:T(8,128)} %copy-done.9) | copy-start | bytes 4718596
  755.5 105.6 %copy-start.25 = (f32[6,32,512]{2,1,0:T(8,128)S(1)}, f32[6,32,512]{2,1,0:T(8,128)}, u32[]{:S(2)}) copy-start(f32[6,32,512]{2,1,0:T(8,128)} %param.41) | copy-start | bytes 1179652
  755.5 105.6 %copy-start.26 = (f32[6,32,512]{2,1,0:T(8,128)S(1)}, f32[6,32,512]{2,1,0:T(8,128)}, u32[]{:S(2)}) copy-start(f32[6,32,512]{2,1,0:T(8,128)} %param.42) | copy-start | bytes 1179652
  1113.8 5.2 copy-start.28
  1113.8 6.2 copy-start.27
  1113.8 7.2 copy-start.13
  1120.0 4.2 slice-start
  1121.0 3.6 slice-start.1
  1121.0 5.7 copy-start.1
  (25 other events, 42.8 us)
Sparse Core Ops, SparseCore 0:
  10.8 48.0 all-gather.4
  150.9 41.7 reduce-scatter.5
  197.1 27.1 all-gather.6
  249.1 43.3 reduce-scatter.7
  301.4 27.1 all-gather.8
  345.5 43.3 reduce-scatter.9
  396.1 27.1 all-gather.10
  736.7 26.1 reduce-scatter.11
  766.8 85.8 reduce-scatter.13
  858.3 255.4 all-reduce.4
